TPU v7x, 256 devices: a whole 4x4x8 slice. The times are simulated.
256 devices in a mesh: zero: 64 (over z, x, core), width: 4 (over y).
Axes of the slice: x: 4, y: 4, z: 8, core: 2. Of those that a mesh axis runs over, the one named last changes fastest.
Arguments:
- weight_up: bfloat16 [12288, 49152], P('zero', 'width'), may hold values from -0.15625 to 0.15625
- low_up: bfloat16 [12288, 64], P('zero'), may hold values from -0.0546875 to 0.0546875
- high_up: bfloat16 [64, 49152], P(None, 'width'), may hold values from -0.75 to 0.75
- norm_train: float32 [12288], P(('zero', 'width')), may hold values from 0.25 to 1.75
- norm_step: float32 [12288], P(('zero', 'width')), may hold values from -0.3 to 0.3
Outputs:
- ready_up: bfloat16 [12288, 49152], P(None, ('width', 'zero'))
- scale_up: float32 [49152], P(('width', 'zero'))
- serve_norm: bfloat16 [12288], replicated
All inputs are finite; a program needn't handle non-finite values. Where the computation divides by a largest or mean magnitude, that divisor is 1e-20 or more.
Results may differ from a plain program's by a relative error of at most 0.001.
Values may be sent and summed in bfloat16 or wider, within the bound.
A program may use at most 128 MiB of HBM per device.

v0:
```python
import functools

import jax
import jax.numpy as jnp
from jax import lax
from jax.sharding import Mesh
from jax.sharding import PartitionSpec as P

ZERO = ("zero_0", "zero_1", "zero_2")
ZERO_WIDTH = ("zero_0", "zero_1", "zero_2", "width")
WIDTH_ZERO = ("width", "zero_0", "zero_1", "zero_2")


mix_rate = 2.0


def by_axis(array, axes):
    return functools.reduce(lax.pmax, axes, array)


def laid_out(parts, dim):
    dims = list(parts.shape[1:])
    dims[dim] *= parts.shape[0]
    return jnp.moveaxis(parts, 0, dim).reshape(dims)


def all_blocks(array, axes, order):
    parts = array[None]
    for k in order:
        parts = lax.all_gather(parts, axes[k], axis=0, tiled=True)
    current = [lax.axis_size(axes[k]) for k in reversed(order)]
    parts = parts.reshape(*current, *array.shape)
    turned = sorted(range(len(order)), key=lambda place: order[len(order) - 1 - place])
    return parts.transpose(*turned, *range(len(order), parts.ndim)).reshape(-1, *array.shape)


def gathered_by_axis(array, axes, order, dim):
    return laid_out(all_blocks(array, axes, order), dim)


def shards(weight_up, low_up, high_up, norm_train, norm_step):
    latest_up = weight_up.astype(jnp.float32) + mix_rate * jnp.dot(
        low_up, high_up, preferred_element_type=jnp.float32
    )
    scale_up = by_axis(jnp.max(jnp.abs(latest_up), axis=0), ZERO)
    narrow_up = (latest_up / scale_up).astype(jnp.bfloat16)
    ready_up = lax.all_to_all(narrow_up, ZERO, split_axis=1, concat_axis=0, tiled=True)
    place = lax.axis_index(ZERO)
    scale_up = lax.dynamic_slice_in_dim(scale_up, place * ready_up.shape[1], ready_up.shape[1])
    serve_norm = gathered_by_axis(
        (norm_train + norm_step).astype(jnp.bfloat16), ZERO_WIDTH, (0, 1, 3, 2), 0
    )
    return (ready_up, scale_up, serve_norm)


def solution(mesh):
    finer = Mesh(
        mesh.devices.reshape(8, 4, 2, mesh.shape["width"]), ("zero_0", "zero_1", "zero_2", "width")
    )
    return jax.shard_map(
        shards,
        mesh=finer,
        in_specs=(P(ZERO, "width"), P(ZERO, None), P(None, "width"), P(ZERO_WIDTH), P(ZERO_WIDTH)),
        out_specs=(P(None, WIDTH_ZERO), P(WIDTH_ZERO), P()),
        check_vma=False,
    )
```

profile of v0, /device:TPU:1, one launch (start us, length us, event | category | flops | bytes accessed | tf_op | source)
XLA Modules:
  0.0 279.0 jit_solution(178411014628912877)
XLA Ops:
  0.6 0.0 copy-start
  0.6 1.4 copy-done
  2.0 7.5 %abs_reduce_fusion = (f32[12288]{0:T(1024)S(1)}, f32[192,12288]{1,0:T(8,128)}) fusion(bf16[192,64]{0,1:T(8,128)(2,1)} %param.6, bf16[64,12288]{1,0:T(8,128)(2,1)S(1)} %copy-done, bf16[192,12288]{1,0:T(8,128)(2,1)} %param.5), kind=kOutput, calls=%fused_computation.3 | convolution fusion | flops 313774080 | bytes 15802368 | tf_op jit(solution)/shard_map/dot_general | solution.py:42
  9.5 27.0 %pmax.21 = f32[12288]{0:T(1024)S(1)} all-reduce(f32[12288]{0:T(1024)S(1)} %get-tuple-element.6), channel_id=1, replica_groups=mesh['zero_0'=8,'zero_1'=4,'zero_2'=2,'width'=4] {'zero_0'}, use_global_device_ids=true, to_apply=%region_1.0 | all-reduce | flops 12288 | bytes 98304 | tf_op jit(solution)/shard_map/pmax | solution.py:18
  36.5 13.6 %pmax.22 = f32[12288]{0:T(1024)S(1)} all-reduce(f32[12288]{0:T(1024)S(1)} %pmax.21), channel_id=1, replica_groups=mesh['zero_0'=8,'zero_1'=4,'zero_2'=2,'width'=4] {'zero_1'}, use_global_device_ids=true, to_apply=%region_2.0 | all-reduce | flops 12288 | bytes 98304 | tf_op jit(solution)/shard_map/pmax | solution.py:18
  50.1 14.8 %pmax.23 = f32[12288]{0:T(1024)S(1)} all-reduce(f32[12288]{0:T(1024)S(1)} %pmax.22), channel_id=1, replica_groups=mesh['zero_0'=8,'zero_1'=4,'zero_2'=2,'width'=4] {'zero_2'}, use_global_device_ids=true, to_apply=%region_3.0 | all-reduce | flops 12288 | bytes 98304 | tf_op jit(solution)/shard_map/pmax | solution.py:18
  64.9 6.6 %divide_convert_fusion = bf16[192,12288]{1,0:T(8,128)(2,1)} fusion(f32[192,12288]{1,0:T(8,128)} %get-tuple-element.7, f32[12288]{0:T(1024)S(1)} %pmax.23), kind=kLoop, calls=%fused_computation.2 | loop fusion | flops 4718592 | bytes 14204928 | tf_op jit(solution)/shard_map/convert_element_type | solution.py:46
  71.5 10.7 %all_to_all.14 = bf16[192,64,192]{2,1,0:T(8,128)(2,1)} reshape(bf16[192,12288]{1,0:T(8,128)(2,1)} %divide_convert_fusion) | data formatting | bytes 9437184 | tf_op jit(solution)/shard_map/all_to_all | solution.py:47
  82.3 9.0 %copy.12 = bf16[192,64,192]{2,0,1:T(8,128)(2,1)} copy(bf16[192,64,192]{2,1,0:T(8,128)(2,1)} %all_to_all.14) | data formatting | bytes 9437184 | tf_op jit(solution)/shard_map/all_to_all | solution.py:47
  91.3 0.0 copy-start.3
  91.3 0.0 copy-start.1
  91.3 0.0 copy-start.2
  91.3 5.5 %all-to-all-start = ((bf16[192,64,192]{2,0,1:T(8,128)(2,1)}), bf16[192,64,192]{2,0,1:T(8,128)(2,1)}, u32[]{:S(2)}, u32[]{:S(2)}) async-start(bf16[192,64,192]{2,0,1:T(8,128)(2,1)} %copy.12), calls=%async_computation | async-start | bytes 12582912 | tf_op jit(solution)/shard_map/all_to_all | solution.py:47
  96.8 0.6 dynamic_slice.3
  97.4 0.0 copy-done.3
  97.4 0.6 dynamic-slice
  98.7 0.0 copy-done.1
  98.7 0.0 copy-done.2
  98.7 0.2 dynamic-update-slice
  99.0 142.0 %all-reduce = bf16[384]{0:T(512)(128)(2,1)S(1)} all-reduce(bf16[384]{0:T(512)(128)(2,1)S(1)} %dynamic-update-slice), channel_id=2, replica_groups=mesh['zero_0'=8,'zero_1'=4,'zero_2'=2,'width'=4] {'zero_0'}, use_global_device_ids=true, to_apply=%add | all-reduce | flops 384 | bytes 1536
  241.0 0.1 reshape.14
  241.1 9.1 %all_gather.13 = bf16[32,48]{1,0:T(8,128)(2,1)S(1)} all-gather(bf16[8,48]{1,0:T(8,128)(2,1)S(1)} %reshape.14), channel_id=1, replica_groups=mesh['zero_0'=8,'zero_1'=4,'zero_2'=2,'width'=4] {'zero_1'}, dimensions={0}, use_global_device_ids=true | all-gather | bytes 3840 | tf_op jit(solution)/shard_map/all_gather | solution.py:30
  250.2 9.5 %all_gather.14 = bf16[128,48]{1,0:T(8,128)(2,1)S(1)} all-gather(bf16[32,48]{1,0:T(8,128)(2,1)S(1)} %all_gather.13), channel_id=1, replica_groups=mesh['zero_0'=8,'zero_1'=4,'zero_2'=2,'width'=4] {'width'}, dimensions={0}, use_global_device_ids=true | all-gather | bytes 15360 | tf_op jit(solution)/shard_map/all_gather | solution.py:30
  259.7 10.5 %all_gather.15 = bf16[256,48]{1,0:T(8,128)(2,1)S(1)} all-gather(bf16[128,48]{1,0:T(8,128)(2,1)S(1)} %all_gather.14), channel_id=1, replica_groups=mesh['zero_0'=8,'zero_1'=4,'zero_2'=2,'width'=4] {'zero_2'}, dimensions={0}, use_global_device_ids=true | all-gather | bytes 36864 | tf_op jit(solution)/shard_map/all_gather | solution.py:30
  270.3 0.7 reshape_reshape.3
  271.1 0.0 all-to-all-done
  271.1 8.0 %copy.14 = bf16[12288,192]{0,1:T(8,128)(2,1)} copy(bf16[12288,192]{1,0:T(8,128)(2,1)} %bitcast.1) | data formatting | bytes 9437184
  (3 shorter events, 0.0 us)
Async XLA Ops:
  0.6 1.4 copy-start
  91.3 6.2 %copy-start.3 = (u32[256]{0:T(256)S(1)}, u32[256]{0:T(256)}, u32[]{:S(2)}) copy-start(u32[256]{0:T(256)} %constant.33) | copy-start | bytes 3076
  91.3 7.4 %copy-start.1 = (f32[48]{0:T(128)S(1)}, f32[48]{0:T(128)}, u32[]{:S(2)}) copy-start(f32[48]{0:T(128)} %param.8) | copy-start | bytes 580
  91.3 7.4 %copy-start.2 = (f32[48]{0:T(128)S(1)}, f32[48]{0:T(128)}, u32[]{:S(2)}) copy-start(f32[48]{0:T(128)} %param.9) | copy-start | bytes 580
  91.3 179.8 %all-to-all-start = ((bf16[192,64,192]{2,0,1:T(8,128)(2,1)}), bf16[192,64,192]{2,0,1:T(8,128)(2,1)}, u32[]{:S(2)}, u32[]{:S(2)}) async-start(bf16[192,64,192]{2,0,1:T(8,128)(2,1)} %copy.12), calls=%async_computation | async-start | bytes 12582912 | tf_op jit(solution)/shard_map/all_to_all | solution.py:47
where the time goes:
time: 280 us; the launch traced here: 279 us
  blocking collectives  227 us (81%)
  local copies, waits for them, and re-layouts  31.5 us (11%)
  matrix products  7.46 us (3%)
  other arithmetic  6.62 us (2%)
  starting transfers between devices  5.48 us (2%)
    unnamed x1, blocking collectives  142 us
    pmax x3, blocking collectives, by_axis(): return functools.reduce(lax.pmax, axes, array)  55.4 us
    all_gather x3, blocking collectives, all_blocks(): parts = lax.all_gather(parts, axes[k], axis=0, tiled=True)  29.2 us
    all_to_all x2, local copies, waits for them, and re-layouts, shards(): lax.all_to_all(narrow_up, ZERO, split_axis=1, concat_axis=0, tiled=True)  19.8 us
    unnamed x12, local copies, waits for them, and re-layouts  10.2 us
    dot_general x1, matrix products, shards(): jnp.dot(low_up, high_up, preferred_element_type=jnp.float32)  7.46 us
    convert_element_type x1, other arithmetic, shards(): narrow_up = (latest_up / scale_up).astype(jnp.bfloat16)  6.62 us
  transfers between devices with their start and end apart: 1, of which 0 were waited for; matrix products, arithmetic and copies ran while one was open for 1% of the time, Pallas kernels for 0%

commit v1 on v0

v1 whole, which is shorter than its diff:
```python
import jax
import jax.numpy as jnp
from jax import lax
from jax.experimental import pallas as pl
from jax.experimental.pallas import tpu as pltpu
from jax.sharding import Mesh
from jax.sharding import PartitionSpec as P

NZ, NX, NC, NW = 8, 4, 2, 4
CHIPS = NZ * NX
MESH = pl.DeviceIdType.MESH
ZERO = ("z", "x", "c")

MIX_RATE = 2.0
STRIDE = 13
FIRST = 5


def gather_kernel(
    weight, low_t, high, train, step,
    latest, tops, norm,
    buf, low_all, norm_all, high_own, high_turned, pick, rows,
    send_sem, full_sem, part_sem, turn_sem, phase_send, phase_recv, local_sem,
):
    z, x, c, w = (lax.axis_index(name) for name in ("z", "x", "c", "w"))
    other = 1 - c
    me = z * NX + x
    depth, rank = weight.shape[0], low_t.shape[0]
    share = rank // NW

    def at(dz=0, dx=0, dw=0, core=c):
        return {
            "z": lax.rem(z + dz + NZ, NZ),
            "x": lax.rem(x + dx + NX, NX),
            "c": core,
            "w": lax.rem(w + dw + NW, NW),
        }

    def shift(k):
        o = lax.rem(k * STRIDE, CHIPS)
        return o // NX, lax.rem(o, NX)

    def remote(src, dst, send, recv, where):
        return pltpu.make_async_remote_copy(
            src_ref=src, dst_ref=dst, send_sem=send, recv_sem=recv, device_id=where, device_id_type=MESH
        )

    barrier = pltpu.get_barrier_semaphore()

    def greet(k, carry):
        dz, dx = shift(k)
        for core in range(NC):
            pl.semaphore_signal(barrier, 1, device_id=at(dz, dx, 0, core), device_id_type=MESH)
        return carry

    lax.fori_loop(1, CHIPS, greet, 0)
    pl.semaphore_signal(barrier, 1, device_id=at(core=other), device_id_type=MESH)
    for dw in range(1, NW):
        pl.semaphore_signal(barrier, 1, device_id=at(dw=dw), device_id_type=MESH)
    pl.semaphore_wait(barrier, NC * (CHIPS - 1) + 1 + NW - 1)

    mine = pl.ds(pl.multiple_of(c * depth, 64), depth)
    part = pl.ds(pl.multiple_of(w * share, 16), share)

    def z_copies():
        out = []
        for i, dz in enumerate(range(1, NZ)):
            out.append(remote(low_t.at[part, :], low_all.at[c, x, z, part, :], phase_send.at[3 * i], phase_recv.at[3 * i], at(dz=dz)))
            out.append(remote(train, norm_all.at[c, x, z, w, 0], phase_send.at[3 * i + 1], phase_recv.at[3 * i + 1], at(dz=dz)))
            out.append(remote(step, norm_all.at[c, x, z, w, 1], phase_send.at[3 * i + 2], phase_recv.at[3 * i + 2], at(dz=dz)))
        return out

    def x_copies():
        out = []
        for i, dx in enumerate(range(1, NX)):
            s = 21 + 2 * i
            here = low_all.at[c, x, :, part, :]
            out.append(remote(here, here, phase_send.at[s], phase_recv.at[s], at(dx=dx)))
            here = norm_all.at[c, x, :, w]
            out.append(remote(here, here, phase_send.at[s + 1], phase_recv.at[s + 1], at(dx=dx)))
        return out

    def y_copies():
        out = []
        for i, dw in enumerate(range(1, NW)):
            s = 27 + 2 * i
            here = low_all.at[c, :, :, part, :]
            out.append(remote(here, here, phase_send.at[s], phase_recv.at[s], at(dw=dw)))
            here = norm_all.at[c, :, :, w]
            out.append(remote(here, here, phase_send.at[s + 1], phase_recv.at[s + 1], at(dw=dw)))
        return out

    def core_copies():
        there = at(core=other)
        return [
            remote(low_all.at[c], low_all.at[c], phase_send.at[33], phase_recv.at[33], there),
            remote(norm_all.at[c], norm_all.at[c], phase_send.at[34], phase_recv.at[34], there),
        ]

    def full_copy(k):
        dz, dx = shift(k)
        there = lax.rem(z + dz, NZ) * NX + lax.rem(x + dx, NX)
        columns = pl.ds(pl.multiple_of(there * 384 + c * 128, 128), 256)
        return remote(weight.at[:, columns], buf.at[me, mine, :], send_sem.at[0], full_sem.at[k], at(dz, dx))

    def part_copy(k):
        dz, dx = shift(k)
        there = lax.rem(z + dz, NZ) * NX + lax.rem(x + dx, NX)
        columns = pl.ds(pl.multiple_of(there * 384 + other * 256, 128), 128)
        lanes = pl.ds(pl.multiple_of(other * 128, 128), 128)
        return remote(weight.at[:, columns], buf.at[me, mine, lanes], send_sem.at[1], part_sem.at[k], at(dz, dx, 0, other))

    def source(k):
        dz, dx = shift(k)
        return lax.rem(z - dz + NZ, NZ), lax.rem(x - dx + NX, NX)

    def turn_copy(k):
        sz, sx = source(k)
        from_chip = sz * NX + sx
        return remote(
            buf.at[from_chip, mine, pl.ds(pl.multiple_of(other * 128, 128), 128)],
            buf.at[from_chip, mine, pl.ds(pl.multiple_of(c * 128, 128), 128)],
            send_sem.at[2], turn_sem.at[k], at(core=other),
        )

    def send(k, carry=0):
        full_copy(k).start()
        part_copy(k).start()
        return carry

    for copy in z_copies():
        copy.start()
    own = [
        pltpu.make_async_copy(weight.at[:, pl.ds(pl.multiple_of(me * 384 + c * 128, 128), 256)], buf.at[me, mine, :], local_sem.at[0]),
        pltpu.make_async_copy(low_t.at[part, :], low_all.at[c, x, z, part, :], local_sem.at[1]),
        pltpu.make_async_copy(train, norm_all.at[c, x, z, w, 0], local_sem.at[2]),
        pltpu.make_async_copy(step, norm_all.at[c, x, z, w, 1], local_sem.at[3]),
        pltpu.make_async_copy(high.at[:, pl.ds(pl.multiple_of(me * 384, 128), 384)], high_own, local_sem.at[4]),
    ]
    for copy in own:
        copy.start()
    lax.fori_loop(1, 1 + FIRST, send, 0)
    part_copy(0).start()

    for copy in own:
        copy.wait()
    turn_copy(0).start()
    high_turned[...] = high_own[...].astype(jnp.float32).T
    column = lax.broadcasted_iota(jnp.int32, pick.shape, 1)
    row = lax.broadcasted_iota(jnp.int32, pick.shape, 0)
    pick[...] = jnp.where(column == row + c * 64, 1.0, 0.0).astype(jnp.bfloat16)
    tops[...] = jnp.zeros_like(tops)

    sent = 1 + FIRST
    before = z_copies()
    for following in (x_copies, y_copies, core_copies):
        for copy in before:
            copy.wait_recv()
        before = following()
        for copy in before:
            copy.start()
        lax.fori_loop(sent, sent + 4, send, 0)
        sent += 4
    for copy in before:
        copy.wait_recv()
    lead = sent - 1

    for core in range(NC):
        for width in range(NW):
            def piece(chip, carry):
                both = norm_all[core, lax.rem(chip, NX), chip // NX, width]
                rows[core * NW + width, pl.ds(chip, 1), :] = both[0] + both[1]
                return carry
            lax.fori_loop(0, CHIPS, piece, 0)
    size = train.shape[1]
    flat = jnp.zeros((CHIPS, 384), jnp.float32)
    for i in range(NC * NW):
        spread = (
            lax.broadcasted_iota(jnp.int32, (size, 384), 1) == lax.broadcasted_iota(jnp.int32, (size, 384), 0) + i * size
        )
        flat += jnp.dot(
            rows[i].astype(jnp.bfloat16), jnp.where(spread, 1.0, 0.0).astype(jnp.bfloat16), preferred_element_type=jnp.float32
        )
    total = jnp.zeros(norm.shape, jnp.float32)
    for t in range(3):
        spread = lax.broadcasted_iota(jnp.int32, (96, CHIPS), 0) == 3 * lax.broadcasted_iota(jnp.int32, (96, CHIPS), 1) + t
        total += jnp.dot(
            jnp.where(spread, 1.0, 0.0).astype(jnp.bfloat16),
            flat[:, t * 128 : (t + 1) * 128].astype(jnp.bfloat16),
            preferred_element_type=jnp.float32,
        )
    norm[...] = total

    def work(k):
        turn_copy(k).wait_recv()
        sz, sx = source(k)
        chip = sz * NX + sx
        factor = high_turned[pl.ds(pl.multiple_of(c * depth, 64), depth), :].astype(jnp.bfloat16)
        base = lax.dot_general(pick[...], buf[chip], (((1,), (1,)), ((), ())), preferred_element_type=jnp.float32)
        change = jnp.concatenate(
            [jnp.dot(factor, low_all[core, sx, sz], preferred_element_type=jnp.float32) for core in range(NC)], axis=1
        )
        value = base + MIX_RATE * change
        latest[:, pl.ds(pl.multiple_of(chip * 384, 128), 384)] = value
        size_of = jnp.abs(value)
        top = jnp.maximum(jnp.maximum(size_of[:, :128], size_of[:, 128:256]), size_of[:, 256:])
        tops[...] = jnp.maximum(tops[...], top)

    part_copy(0).wait_recv()

    def main(k, carry):
        full_copy(k).wait_recv()
        part_copy(k).wait_recv()
        turn_copy(k).start()

        @pl.when(k + lead < CHIPS)
        def _():
            send(k + lead)

        work(k - 1)
        return carry

    lax.fori_loop(1, CHIPS, main, 0)
    work(CHIPS - 1)

    for copies in (z_copies, x_copies, y_copies, core_copies):
        for copy in copies():
            copy.wait_send()
    for i, of in enumerate(
        (buf.at[pl.ds(0, CHIPS - 1), pl.ds(0, depth), :], buf.at[:, pl.ds(0, depth), pl.ds(0, 128)], buf.at[:, pl.ds(0, depth), pl.ds(0, 128)])
    ):
        pltpu.make_async_copy(of, of, send_sem.at[i]).wait()


def scale_kernel(latest, tops, norm, ready, scale, serve, narrow, sems):
    top = jnp.max(tops[...], axis=1, keepdims=True)
    scale[...] = jnp.max(tops[...].T, axis=0, keepdims=True)
    serve[...] = norm[...].astype(jnp.bfloat16)
    inverse = 1.0 / top
    block = 16
    copies = []
    for i in range(latest.shape[0] // block):
        at = pl.ds(i * block, block)
        narrow[at, :] = (latest[at, :] * inverse[i * block : (i + 1) * block]).astype(jnp.bfloat16)
        copy = pltpu.make_async_copy(narrow.at[at, :], ready.at[at, :], sems.at[i])
        copy.start()
        copies.append(copy)
    for copy in copies:
        copy.wait()


def shards(weight_up, low_up, high_up, norm_train, norm_step):
    depth, inner = weight_up.shape
    rank = low_up.shape[1]
    piece = norm_train.shape[0]
    anywhere = pl.BlockSpec(memory_space=pltpu.HBM)
    in_vmem = pl.BlockSpec(memory_space=pltpu.VMEM)
    latest, tops, norm = pl.pallas_call(
        gather_kernel,
        out_shape=(
            jax.ShapeDtypeStruct((depth, inner), jnp.float32),
            jax.ShapeDtypeStruct((depth, 128), jnp.float32),
            jax.ShapeDtypeStruct((96, 128), jnp.float32),
        ),
        in_specs=[anywhere] * 5,
        out_specs=(in_vmem,) * 3,
        scratch_shapes=[
            pltpu.VMEM((CHIPS, 2 * depth, 256), jnp.bfloat16),
            pltpu.VMEM((NC, NX, NZ, rank, depth), jnp.bfloat16),
            pltpu.VMEM((NC, NX, NZ, NW, 2, 1, piece), jnp.float32),
            pltpu.VMEM((rank, 384), jnp.bfloat16),
            pltpu.VMEM((384, rank), jnp.float32),
            pltpu.VMEM((depth, 256), jnp.bfloat16),
            pltpu.VMEM((NC * NW, CHIPS, piece), jnp.float32),
            pltpu.SemaphoreType.DMA((3,)),
            pltpu.SemaphoreType.DMA((CHIPS,)),
            pltpu.SemaphoreType.DMA((CHIPS,)),
            pltpu.SemaphoreType.DMA((CHIPS,)),
            pltpu.SemaphoreType.DMA((35,)),
            pltpu.SemaphoreType.DMA((35,)),
            pltpu.SemaphoreType.DMA((5,)),
        ],
        compiler_params=pltpu.CompilerParams(collective_id=0, has_side_effects=True, vmem_limit_bytes=28 * 1024 * 1024),
        name="gather",
    )(weight_up, low_up.T, high_up, norm_train.reshape(1, piece), norm_step.reshape(1, piece))
    ready, scale, serve = pl.pallas_call(
        scale_kernel,
        out_shape=(
            jax.ShapeDtypeStruct((depth, inner), jnp.bfloat16),
            jax.ShapeDtypeStruct((1, depth), jnp.float32),
            jax.ShapeDtypeStruct((96, 128), jnp.bfloat16),
        ),
        in_specs=[in_vmem] * 3,
        out_specs=(anywhere, in_vmem, in_vmem),
        scratch_shapes=[pltpu.VMEM((depth, inner), jnp.bfloat16), pltpu.SemaphoreType.DMA((depth // 16,))],
        compiler_params=pltpu.CompilerParams(vmem_limit_bytes=28 * 1024 * 1024),
        name="scale",
    )(latest, tops, norm)
    return ready.T, scale.reshape(depth), serve.reshape(96 * 128)


def solution(mesh):
    finer = Mesh(mesh.devices.reshape(NZ, NX, NC, NW), ("z", "x", "c", "w"))
    return jax.shard_map(
        shards,
        mesh=finer,
        in_specs=(P(ZERO, "w"), P(ZERO, None), P(None, "w"), P(ZERO + ("w",)), P(ZERO + ("w",))),
        out_specs=(P(None, ("w",) + ZERO), P(("w",) + ZERO), P()),
        check_vma=False,
    )
```

time: 280 us -> 129 us (0.46)
  blocking collectives: 227 us -> 0 us
  Pallas kernels: 0 us -> 123 us
  local copies, waits for them, and re-layouts: 31.5 us -> 5.8 us
  matrix products: 7.46 us -> 0 us
  other arithmetic: 6.62 us -> 0 us
  starting transfers between devices: 5.48 us -> 0 us
    unnamed x1 -> x0, blocking collectives: 142 us -> none
    pallas_call x0 -> x2, Pallas kernels: none -> 123 us  [the longest x1 120 us: shards(): pl.pallas_call(gather_kernel, out_shape=(jax.ShapeDtypeStruct((depth, inn...]
    pmax x3 -> x0, blocking collectives: 55.4 us -> none  [by_axis(): return functools.reduce(lax.pmax, axes, array)]
    all_gather x3 -> x0, blocking collectives: 29.2 us -> none  [all_blocks(): parts = lax.all_gather(parts, axes[k], axis=0, tiled=True)]
    all_to_all x2 -> x0, local copies, waits for them, and re-layouts: 19.8 us -> none  [shards(): lax.all_to_all(narrow_up, ZERO, split_axis=1, concat_axis=0, tiled=True)]
    dot_general x1 -> x0, matrix products: 7.46 us -> none  [shards(): jnp.dot(low_up, high_up, preferred_element_type=jnp.float32)]
    convert_element_type x2 -> x0, other arithmetic: 6.62 us -> none  [the longest x1 6.62 us: shards(): narrow_up = (latest_up / scale_up).astype(jnp.bfloat16)]
    all_to_all x1 -> x0, starting transfers between devices: 5.48 us -> none  [shards(): lax.all_to_all(narrow_up, ZERO, split_axis=1, concat_axis=0, tiled=True)]
  transfers between devices with their start and end apart: 1 -> 0, of which waited for: 0 -> 0; matrix products, arithmetic and copies ran while one was open for 1% -> 0% of each run, Pallas kernels for 0% -> 0%
where the time goes in v1:
time: 129 us
  Pallas kernels  123 us (95%)
  local copies, waits for them, and re-layouts  5.8 us (4%)
    pallas_call x1, Pallas kernels, shards(): pl.pallas_call(gather_kernel, out_shape=(jax.ShapeDtypeStruct((depth, inn...  120 us
    unnamed x10, local copies, waits for them, and re-layouts  5.8 us
    pallas_call x1, Pallas kernels, shards(): pl.pallas_call(scale_kernel, out_shape=(jax.ShapeDtypeStruct((depth, inne...  3.1 us

profile of v1, /device:TPU:1, one launch (start us, length us, event | category | flops | bytes accessed | tf_op | source)
XLA Modules:
  0.0 129.1 jit_solution(17041653313994730787)
XLA Ops:
  0.6 0.0 copy-start
  0.6 2.3 %copy-done = bf16[192,12288]{1,0:T(8,128)(2,1)S(1)} copy-done((bf16[192,12288]{1,0:T(8,128)(2,1)S(1)}, bf16[192,12288]{1,0:T(8,128)(2,1)}, u32[]{:S(2)}) %copy-start) | copy-done | bytes 4718616
  3.0 0.0 copy-start.1
  3.0 1.4 %copy-done.1 = bf16[64,12288]{1,0:T(8,128)(2,1)S(1)} copy-done((bf16[64,12288]{1,0:T(8,128)(2,1)S(1)}, bf16[64,12288]{1,0:T(8,128)(2,1)}, u32[]{:S(2)}) %copy-start.1) | copy-done | bytes 1572888
  4.4 0.0 copy-start.2
  4.4 0.8 copy-done.2
  5.1 0.0 copy-start.3
  5.1 0.7 copy-done.3
  5.8 0.0 copy-start.4
  5.8 0.7 copy-done.4
  6.4 119.6 %gather.1 = (f32[192,12288]{1,0:T(8,128)S(1)}, f32[192,128]{1,0:T(8,128)S(1)}, f32[96,128]{1,0:T(8,128)S(1)}) custom-call(bf16[192,12288]{1,0:T(8,128)(2,1)S(1)} %copy-done, bf16[64,192]{1,0:T(8,128)(2,1)S(1)} %bitcast.6, bf16[64,12288]{1,0:T(8,128)(2,1)S(1)} %copy-done.1, f32[1,48]{1,0:T(1,128)S(1)} %bitcast.7, f32[1,48]{1,0:T(1,128)S(1)} %bitcast.8), custom_call_target="tpu_custom_call" | custom-call | tf_op jit(solution)/shard_map/gather/pallas_call | solution.py:258
  126.0 3.1 %scale.1 = (bf16[192,12288]{1,0:T(8,128)(2,1)}, f32[1,192]{1,0:T(1,128)}, bf16[96,128]{1,0:T(8,128)(2,1)}) custom-call(f32[192,12288]{1,0:T(8,128)S(1)} %get-tuple-element.9.latest, f32[192,128]{1,0:T(8,128)S(1)} %get-tuple-element.10.tops, f32[96,128]{1,0:T(8,128)S(1)} %get-tuple-element.11.norm), custom_call_target="tpu_custom_call" | custom-call | tf_op jit(solution)/shard_map/scale/pallas_call | solution.py:286
Async XLA Ops:
  0.6 2.3 %copy-start = (bf16[192,12288]{1,0:T(8,128)(2,1)S(1)}, bf16[192,12288]{1,0:T(8,128)(2,1)}, u32[]{:S(2)}) copy-start(bf16[192,12288]{1,0:T(8,128)(2,1)} %weight.1) | copy-start | bytes 14155780
  3.0 1.4 %copy-start.1 = (bf16[64,12288]{1,0:T(8,128)(2,1)S(1)}, bf16[64,12288]{1,0:T(8,128)(2,1)}, u32[]{:S(2)}) copy-start(bf16[64,12288]{1,0:T(8,128)(2,1)} %high.1) | copy-start | bytes 4718596
  4.4 0.8 copy-start.2
  5.1 0.7 copy-start.3
  5.8 0.7 copy-start.4

commit v2 on v1

--- a/solution.py
+++ b/solution.py
@@ -282,7 +282,12 @@
         ],
         compiler_params=pltpu.CompilerParams(collective_id=0, has_side_effects=True, vmem_limit_bytes=28 * 1024 * 1024),
         name="gather",
-    )(weight_up, low_up.T, high_up, norm_train.reshape(1, piece), norm_step.reshape(1, piece))
+    )(
+        *(
+            pltpu.with_memory_space_constraint(operand, pltpu.HBM)
+            for operand in (weight_up, low_up.T, high_up, norm_train.reshape(1, piece), norm_step.reshape(1, piece))
+        )
+    )
     ready, scale, serve = pl.pallas_call(
         scale_kernel,
         out_shape=(

time: 129 us -> 125 us (0.969)
  local copies, waits for them, and re-layouts: 5.8 us -> 0 us
    unnamed x10 -> x0, local copies, waits for them, and re-layouts: 5.8 us -> none
where the time goes in v2:
time: 125 us; the launch traced here: 124 us
  Pallas kernels  124 us (99%)
    pallas_call x1, Pallas kernels, shards(): pl.pallas_call(gather_kernel, out_shape=(jax.ShapeDtypeStruct((depth, inn...  121 us
    pallas_call x1, Pallas kernels, shards(): pl.pallas_call(scale_kernel, out_shape=(jax.ShapeDtypeStruct((depth, inne...  3.1 us

profile of v2, /device:TPU:1, one launch (start us, length us, event | category | flops | bytes accessed | tf_op | source)
XLA Modules:
  0.0 124.4 jit_solution(3456156281273266921)
XLA Ops:
  0.6 120.7 %gather.1 = (f32[192,12288]{1,0:T(8,128)S(1)}, f32[192,128]{1,0:T(8,128)S(1)}, f32[96,128]{1,0:T(8,128)S(1)}) custom-call(bf16[192,12288]{1,0:T(8,128)(2,1)} %weight.1, bf16[64,192]{1,0:T(8,128)(2,1)} %bitcast.6, bf16[64,12288]{1,0:T(8,128)(2,1)} %high.1, f32[1,48]{1,0:T(1,128)} %bitcast.7, f32[1,48]{1,0:T(1,128)} %bitcast.8), custom_call_target="tpu_custom_call" | custom-call | tf_op jit(solution)/shard_map/gather/pallas_call | solution.py:258
  121.3 3.1 %scale.1 = (bf16[192,12288]{1,0:T(8,128)(2,1)}, f32[1,192]{1,0:T(1,128)}, bf16[96,128]{1,0:T(8,128)(2,1)}) custom-call(f32[192,12288]{1,0:T(8,128)S(1)} %get-tuple-element.9.latest, f32[192,128]{1,0:T(8,128)S(1)} %get-tuple-element.10.tops, f32[96,128]{1,0:T(8,128)S(1)} %get-tuple-element.11.norm), custom_call_target="tpu_custom_call" | custom-call | tf_op jit(solution)/shard_map/scale/pallas_call | solution.py:291

commit v3 on v2

v3 whole, which is shorter than its diff:
```python
import jax
import jax.numpy as jnp
from jax import lax
from jax.experimental import pallas as pl
from jax.experimental.pallas import tpu as pltpu
from jax.sharding import Mesh
from jax.sharding import PartitionSpec as P

NZ, NX, NC, NW = 8, 4, 2, 4
CHIPS = NZ * NX
MESH = pl.DeviceIdType.MESH
ZERO = ("z", "x", "c")

MIX_RATE = 2.0
ORDER = (0, 1, 4, 28, 3, 13, 26, 7, 20, 14, 27, 8, 21, 2, 15, 9, 22, 16, 29, 10, 23, 17, 30, 11, 24, 5, 18, 31, 12, 25, 6, 19)
FIRST = 4
MORE = (0, 0, 5, 5, 17, 0)


def gather_kernel(
    weight, low_t, high, train, step,
    latest, tops, norm,
    buf, low_all, norm_all, high_own, high_turned, pick, rows,
    send_sem, block_sem, turn_sem, phase_send, phase_recv, round_sem, local_sem,
):
    z, x, c, w = (lax.axis_index(name) for name in ("z", "x", "c", "w"))
    other = 1 - c
    me = z * NX + x
    depth, rank = weight.shape[0], low_t.shape[0]
    share = rank // NW

    def at(dz=0, dx=0, dw=0, core=c):
        return {
            "z": lax.rem(z + dz + NZ, NZ),
            "x": lax.rem(x + dx + NX, NX),
            "c": core,
            "w": lax.rem(w + dw + NW, NW),
        }

    def shift(k):
        word, place = k // 6, lax.rem(k, 6)
        packed, below = jnp.int32(0), jnp.int32(1)
        for i in range(6):
            packed = jnp.where(word == i, sum(o << 5 * n for n, o in enumerate(ORDER[6 * i : 6 * i + 6])), packed)
            below = jnp.where(place == i, 1 << 5 * i, below)
        o = lax.rem(packed // below, 32)
        return o // NX, lax.rem(o, NX)

    def remote(src, dst, send, recv, where):
        return pltpu.make_async_remote_copy(
            src_ref=src, dst_ref=dst, send_sem=send, recv_sem=recv, device_id=where, device_id_type=MESH
        )

    barrier = pltpu.get_barrier_semaphore()
    near = [(dz, dx, 0, core) for dz in (1, NZ - 1) for dx in range(NX) for core in (c, other)]
    near += [(0, dx, 0, core) for dx in range(1, NX) for core in (c, other)]
    near += [(0, 0, 0, other)] + [(0, 0, dw, c) for dw in range(1, NW)]
    for where in near:
        pl.semaphore_signal(barrier, 1, device_id=at(*where), device_id_type=MESH)
    pl.semaphore_wait(barrier, len(near))

    def tell(r):
        for dz in (1, NZ - 1):
            pl.semaphore_signal(round_sem.at[r], 1, device_id=at(dz), device_id_type=MESH)

    def hear(r):
        pl.semaphore_wait(round_sem.at[r], 2)

    mine = pl.ds(pl.multiple_of(c * depth, 64), depth)
    part = pl.ds(pl.multiple_of(w * share, 16), share)

    def pair(phase, low_from, low_to, norm_from, norm_to, where):
        return [
            remote(low_from, low_to, phase_send.at[phase, 0], phase_recv.at[phase, 0], where),
        ] + [remote(a, b, phase_send.at[phase, 1], phase_recv.at[phase, 1], where) for a, b in zip(norm_from, norm_to)]

    def z_copies(dz):
        here = norm_all.at[c, x, z, w]
        return pair(0, low_t.at[part, :], low_all.at[c, x, z, part, :], (train, step), (here.at[0], here.at[1]), at(dz))

    def x_copies():
        low, gain = low_all.at[c, x, :, part, :], norm_all.at[c, x, :, w]
        return [copy for dx in range(1, NX) for copy in pair(1, low, low, (gain,), (gain,), at(0, dx))]

    def y_copies():
        low, gain = low_all.at[c, :, :, part, :], norm_all.at[c, :, :, w]
        return [copy for dw in range(1, NW) for copy in pair(2, low, low, (gain,), (gain,), at(dw=dw))]

    def core_copies():
        return pair(3, low_all.at[c], low_all.at[c], (norm_all.at[c],), (norm_all.at[c],), at(core=other))

    bytes_of = (
        (low_all.at[0, 0, pl.ds(0, NZ - 1), part, :], norm_all.at[0, 0, pl.ds(0, NZ - 1), 0]),
        (low_all.at[0, pl.ds(0, NX - 1), :, part, :], norm_all.at[0, pl.ds(0, NX - 1), :, 0]),
        (low_all.at[0, :, :, pl.ds(0, share * (NW - 1)), :], norm_all.at[0, :, :, pl.ds(0, NW - 1)]),
        (low_all.at[0], norm_all.at[0]),
    )

    def wait_bytes(of, sem):
        pltpu.make_async_copy(of, of, sem).wait()

    def wait_phase(phase, sems):
        for kind in range(2):
            wait_bytes(bytes_of[phase][kind], sems.at[phase, kind])

    def full_copy(k):
        dz, dx = shift(k)
        there = lax.rem(z + dz, NZ) * NX + lax.rem(x + dx, NX)
        columns = pl.ds(pl.multiple_of(there * 384 + c * 128, 128), 256)
        return remote(weight.at[:, columns], buf.at[me, mine, :], send_sem.at[0], block_sem.at[k], at(dz, dx))

    def part_copy(k):
        dz, dx = shift(k)
        there = lax.rem(z + dz, NZ) * NX + lax.rem(x + dx, NX)
        columns = pl.ds(pl.multiple_of(there * 384 + other * 256, 128), 128)
        lanes = pl.ds(pl.multiple_of(other * 128, 128), 128)
        return remote(weight.at[:, columns], buf.at[me, mine, lanes], send_sem.at[1], block_sem.at[k], at(dz, dx, 0, other))

    def source(k):
        dz, dx = shift(k)
        return lax.rem(z - dz + NZ, NZ), lax.rem(x - dx + NX, NX)

    def turn_copy(k):
        sz, sx = source(k)
        from_chip = sz * NX + sx
        return remote(
            buf.at[from_chip, mine, pl.ds(pl.multiple_of(other * 128, 128), 128)],
            buf.at[from_chip, mine, pl.ds(pl.multiple_of(c * 128, 128), 128)],
            send_sem.at[1], turn_sem.at[lax.rem(k, 4)], at(core=other),
        )

    def send(k, carry=0):
        full_copy(k).start()
        part_copy(k).start()
        return carry

    own = [
        pltpu.make_async_copy(weight.at[:, pl.ds(pl.multiple_of(me * 384 + c * 128, 128), 256)], buf.at[me, mine, :], local_sem.at[0]),
        pltpu.make_async_copy(low_t.at[part, :], low_all.at[c, x, z, part, :], local_sem.at[1]),
        pltpu.make_async_copy(high.at[:, pl.ds(pl.multiple_of(me * 384, 128), 384)], high_own, local_sem.at[2]),
        pltpu.make_async_copy(train, norm_all.at[c, x, z, w, 0], local_sem.at[3]),
        pltpu.make_async_copy(step, norm_all.at[c, x, z, w, 1], local_sem.at[4]),
    ]
    sent = 1

    def send_more(count):
        nonlocal sent
        lax.fori_loop(sent, sent + count, send, 0)
        sent += count

    tell(0)
    for dz in (1, NZ - 1):
        for copy in z_copies(dz):
            copy.start()
    send_more(FIRST)
    for copy in own:
        copy.start()
    for r in range(3):
        hear(r)
        if r < 2:
            tell(r + 1)
        for dz in sorted({2 + r, NZ - 2 - r}):
            for copy in z_copies(dz):
                copy.start()
        send_more(MORE[r])
    part_copy(0).start()

    for copy in own:
        copy.wait()
    turn_copy(0).start()
    high_turned[...] = high_own[...].astype(jnp.float32).T
    column = lax.broadcasted_iota(jnp.int32, pick.shape, 1)
    row = lax.broadcasted_iota(jnp.int32, pick.shape, 0)
    pick[...] = jnp.where(column == row + c * 64, 1.0, 0.0).astype(jnp.bfloat16)
    tops[...] = jnp.zeros_like(tops)

    for phase, following in enumerate((x_copies, y_copies, core_copies)):
        wait_phase(phase, phase_recv)
        for copy in following():
            copy.start()
        send_more(MORE[3 + phase])
    wait_phase(3, phase_recv)
    lead = sent - 1

    for core in range(NC):
        for width in range(NW):
            def piece(chip, carry):
                both = norm_all[core, lax.rem(chip, NX), chip // NX, width]
                rows[core * NW + width, pl.ds(chip, 1), :] = both[0] + both[1]
                return carry
            lax.fori_loop(0, CHIPS, piece, 0)
    size = train.shape[1]
    flat = jnp.zeros((CHIPS, 384), jnp.float32)
    for i in range(NC * NW):
        spread = (
            lax.broadcasted_iota(jnp.int32, (size, 384), 1) == lax.broadcasted_iota(jnp.int32, (size, 384), 0) + i * size
        )
        flat += jnp.dot(
            rows[i].astype(jnp.bfloat16), jnp.where(spread, 1.0, 0.0).astype(jnp.bfloat16), preferred_element_type=jnp.float32
        )
    total = jnp.zeros(norm.shape, jnp.float32)
    for t in range(3):
        spread = lax.broadcasted_iota(jnp.int32, (96, CHIPS), 0) == 3 * lax.broadcasted_iota(jnp.int32, (96, CHIPS), 1) + t
        total += jnp.dot(
            jnp.where(spread, 1.0, 0.0).astype(jnp.bfloat16),
            flat[:, t * 128 : (t + 1) * 128].astype(jnp.bfloat16),
            preferred_element_type=jnp.float32,
        )
    norm[...] = total

    def work(k):
        turn_copy(k).wait_recv()
        sz, sx = source(k)
        chip = sz * NX + sx
        factor = high_turned[pl.ds(pl.multiple_of(c * depth, 64), depth), :].astype(jnp.bfloat16)
        base = lax.dot_general(pick[...], buf[chip], (((1,), (1,)), ((), ())), preferred_element_type=jnp.float32)
        change = jnp.concatenate(
            [jnp.dot(factor, low_all[core, sx, sz], preferred_element_type=jnp.float32) for core in range(NC)], axis=1
        )
        value = base + MIX_RATE * change
        latest[:, pl.ds(pl.multiple_of(chip * 384, 128), 384)] = value
        size_of = jnp.abs(value)
        top = jnp.maximum(jnp.maximum(size_of[:, :128], size_of[:, 128:256]), size_of[:, 256:])
        tops[...] = jnp.maximum(tops[...], top)

    wait_bytes(buf.at[0, pl.ds(0, depth), pl.ds(0, 128)], block_sem.at[0])

    def main(k, carry):
        wait_bytes(buf.at[0, pl.ds(0, depth * 3 // 2), :], block_sem.at[k])
        turn_copy(k).start()

        @pl.when(k + lead < CHIPS)
        def _():
            send(k + lead)

        work(k - 1)
        return carry

    lax.fori_loop(1, CHIPS, main, 0)
    work(CHIPS - 1)

    for phase in range(4):
        wait_phase(phase, phase_send)
    wait_bytes(buf.at[pl.ds(0, CHIPS - 1), pl.ds(0, depth), :], send_sem.at[0])
    wait_bytes(buf.at[:, pl.ds(0, depth), :], send_sem.at[1])


def scale_kernel(latest, tops, norm, ready, scale, serve, narrow, scale_row, serve_rows, sems):
    top = jnp.max(tops[...], axis=1, keepdims=True)
    inverse = 1.0 / top
    block = 16
    copies = []
    for i in range(latest.shape[0] // block):
        at = pl.ds(i * block, block)
        narrow[at, :] = (latest[at, :] * inverse[i * block : (i + 1) * block]).astype(jnp.bfloat16)
        copies.append(pltpu.make_async_copy(narrow.at[at, :], ready.at[at, :], sems.at[i]))
        copies[-1].start()
        if i == 0:
            scale_row[...] = jnp.max(tops[...].T, axis=0, keepdims=True)
            serve_rows[...] = norm[...].astype(jnp.bfloat16)
            copies.append(pltpu.make_async_copy(scale_row, scale, sems.at[latest.shape[0] // block]))
            copies[-1].start()
            copies.append(pltpu.make_async_copy(serve_rows, serve, sems.at[latest.shape[0] // block + 1]))
            copies[-1].start()
    for copy in copies:
        copy.wait()


def shards(weight_up, low_up, high_up, norm_train, norm_step):
    depth, inner = weight_up.shape
    rank = low_up.shape[1]
    piece = norm_train.shape[0]
    anywhere = pl.BlockSpec(memory_space=pltpu.HBM)
    in_vmem = pl.BlockSpec(memory_space=pltpu.VMEM)
    latest, tops, norm = pl.pallas_call(
        gather_kernel,
        out_shape=(
            jax.ShapeDtypeStruct((depth, inner), jnp.float32),
            jax.ShapeDtypeStruct((depth, 128), jnp.float32),
            jax.ShapeDtypeStruct((96, 128), jnp.float32),
        ),
        in_specs=[anywhere] * 5,
        out_specs=(in_vmem,) * 3,
        scratch_shapes=[
            pltpu.VMEM((CHIPS, 2 * depth, 256), jnp.bfloat16),
            pltpu.VMEM((NC, NX, NZ, rank, depth), jnp.bfloat16),
            pltpu.VMEM((NC, NX, NZ, NW, 2, 1, piece), jnp.float32),
            pltpu.VMEM((rank, 384), jnp.bfloat16),
            pltpu.VMEM((384, rank), jnp.float32),
            pltpu.VMEM((depth, 256), jnp.bfloat16),
            pltpu.VMEM((NC * NW, CHIPS, piece), jnp.float32),
            pltpu.SemaphoreType.DMA((2,)),
            pltpu.SemaphoreType.DMA((CHIPS,)),
            pltpu.SemaphoreType.DMA((4,)),
            pltpu.SemaphoreType.DMA((4, 2)),
            pltpu.SemaphoreType.DMA((4, 2)),
            pltpu.SemaphoreType.REGULAR((3,)),
            pltpu.SemaphoreType.DMA((5,)),
        ],
        compiler_params=pltpu.CompilerParams(collective_id=0, has_side_effects=True, vmem_limit_bytes=28 * 1024 * 1024),
        name="gather",
    )(
        *(
            pltpu.with_memory_space_constraint(operand, pltpu.HBM)
            for operand in (weight_up, low_up.T, high_up, norm_train.reshape(1, piece), norm_step.reshape(1, piece))
        )
    )
    ready, scale, serve = pl.pallas_call(
        scale_kernel,
        out_shape=(
            jax.ShapeDtypeStruct((depth, inner), jnp.bfloat16),
            jax.ShapeDtypeStruct((1, depth), jnp.float32),
            jax.ShapeDtypeStruct((96, 128), jnp.bfloat16),
        ),
        in_specs=[in_vmem] * 3,
        out_specs=(anywhere,) * 3,
        scratch_shapes=[
            pltpu.VMEM((depth, inner), jnp.bfloat16),
            pltpu.VMEM((1, depth), jnp.float32),
            pltpu.VMEM((96, 128), jnp.bfloat16),
            pltpu.SemaphoreType.DMA((depth // 16 + 2,)),
        ],
        compiler_params=pltpu.CompilerParams(vmem_limit_bytes=28 * 1024 * 1024),
        name="scale",
    )(latest, tops, norm)
    return ready.T, scale.reshape(depth), serve.reshape(96 * 128)


def solution(mesh):
    finer = Mesh(mesh.devices.reshape(NZ, NX, NC, NW), ("z", "x", "c", "w"))
    return jax.shard_map(
        shards,
        mesh=finer,
        in_specs=(P(ZERO, "w"), P(ZERO, None), P(None, "w"), P(ZERO + ("w",)), P(ZERO + ("w",))),
        out_specs=(P(None, ("w",) + ZERO), P(("w",) + ZERO), P()),
        check_vma=False,
    )
```

time: 125 us -> 120 us (0.960)
  Pallas kernels: 124 us -> 118 us
    pallas_call x1, Pallas kernels: 121 us -> 116 us  [shards(): pl.pallas_call(gather_kernel, out_shape=(jax.ShapeDtypeStruct((depth, inn...]
where the time goes in v3:
time: 120 us; the launch traced here: 119 us
  Pallas kernels  118 us (98%)
    pallas_call x1, Pallas kernels, shards(): pl.pallas_call(gather_kernel, out_shape=(jax.ShapeDtypeStruct((depth, inn...  116 us
    pallas_call x1, Pallas kernels, shards(): pl.pallas_call(scale_kernel, out_shape=(jax.ShapeDtypeStruct((depth, inne...  2.46 us

profile of v3, /device:TPU:1, one launch (start us, length us, event | category | flops | bytes accessed | tf_op | source)
XLA Modules:
  0.0 118.9 jit_solution(9919116174556965153)
XLA Ops:
  0.6 115.8 %gather.1 = (f32[192,12288]{1,0:T(8,128)S(1)}, f32[192,128]{1,0:T(8,128)S(1)}, f32[96,128]{1,0:T(8,128)S(1)}) custom-call(bf16[192,12288]{1,0:T(8,128)(2,1)} %weight.1, bf16[64,192]{1,0:T(8,128)(2,1)} %bitcast.6, bf16[64,12288]{1,0:T(8,128)(2,1)} %high.1, f32[1,48]{1,0:T(1,128)} %bitcast.7, f32[1,48]{1,0:T(1,128)} %bitcast.8), custom_call_target="tpu_custom_call" | custom-call | tf_op jit(solution)/shard_map/gather/pallas_call | solution.py:275
  116.4 2.5 %scale.1 = (bf16[192,12288]{1,0:T(8,128)(2,1)}, f32[1,192]{1,0:T(1,128)}, bf16[96,128]{1,0:T(8,128)(2,1)}) custom-call(f32[192,12288]{1,0:T(8,128)S(1)} %get-tuple-element.9.latest, f32[192,128]{1,0:T(8,128)S(1)} %get-tuple-element.10.tops, f32[96,128]{1,0:T(8,128)S(1)} %get-tuple-element.11.norm), custom_call_target="tpu_custom_call" | custom-call | tf_op jit(solution)/shard_map/scale/pallas_call | solution.py:308

commit v4 on v3

--- a/solution.py
+++ b/solution.py
@@ -14,7 +14,7 @@
 MIX_RATE = 2.0
 ORDER = (0, 1, 4, 28, 3, 13, 26, 7, 20, 14, 27, 8, 21, 2, 15, 9, 22, 16, 29, 10, 23, 17, 30, 11, 24, 5, 18, 31, 12, 25, 6, 19)
 FIRST = 4
-MORE = (0, 0, 5, 5, 17, 0)
+MORE = (0, 0, 5, 22, 0, 0)
 
 
 def gather_kernel(
@@ -71,8 +71,8 @@
 
     def pair(phase, low_from, low_to, norm_from, norm_to, where):
         return [
-            remote(low_from, low_to, phase_send.at[phase, 0], phase_recv.at[phase, 0], where),
-        ] + [remote(a, b, phase_send.at[phase, 1], phase_recv.at[phase, 1], where) for a, b in zip(norm_from, norm_to)]
+            remote(low_from, low_to, phase_send.at[phase % 2, 0], phase_recv.at[phase, 0], where),
+        ] + [remote(a, b, phase_send.at[phase % 2, 1], phase_recv.at[phase, 1], where) for a, b in zip(norm_from, norm_to)]
 
     def z_copies(dz):
         here = norm_all.at[c, x, z, w]
@@ -101,7 +101,7 @@
 
     def wait_phase(phase, sems):
         for kind in range(2):
-            wait_bytes(bytes_of[phase][kind], sems.at[phase, kind])
+            wait_bytes(bytes_of[phase][kind], sems.at[phase % sems.shape[0], kind])
 
     def full_copy(k):
         dz, dx = shift(k)
@@ -176,6 +176,8 @@
 
     for phase, following in enumerate((x_copies, y_copies, core_copies)):
         wait_phase(phase, phase_recv)
+        if phase > 0:
+            wait_phase(phase - 1, phase_send)
         for copy in following():
             copy.start()
         send_more(MORE[3 + phase])
@@ -208,22 +210,30 @@
         )
     norm[...] = total
 
-    def work(k):
-        turn_copy(k).wait_recv()
+    def work(k, row, count, lane):
         sz, sx = source(k)
         chip = sz * NX + sx
-        factor = high_turned[pl.ds(pl.multiple_of(c * depth, 64), depth), :].astype(jnp.bfloat16)
-        base = lax.dot_general(pick[...], buf[chip], (((1,), (1,)), ((), ())), preferred_element_type=jnp.float32)
+        out, lanes = pl.ds(pl.multiple_of(row, 64), count), pl.ds(pl.multiple_of(lane, 128), 128)
+        factor = high_turned[pl.ds(pl.multiple_of(c * depth + row, 64), count), :].astype(jnp.bfloat16)
+        base = lax.dot_general(pick[out, lanes], buf[chip, :, lanes], (((1,), (1,)), ((), ())), preferred_element_type=jnp.float32)
         change = jnp.concatenate(
             [jnp.dot(factor, low_all[core, sx, sz], preferred_element_type=jnp.float32) for core in range(NC)], axis=1
         )
         value = base + MIX_RATE * change
-        latest[:, pl.ds(pl.multiple_of(chip * 384, 128), 384)] = value
+        latest[out, pl.ds(pl.multiple_of(chip * 384, 128), 384)] = value
         size_of = jnp.abs(value)
         top = jnp.maximum(jnp.maximum(size_of[:, :128], size_of[:, 128:256]), size_of[:, 256:])
-        tops[...] = jnp.maximum(tops[...], top)
+        tops[out, :] = jnp.maximum(tops[out, :], top)
+
+    def work_own(k):
+        work(k, c * 64, 128, c * 128)
+
+    def work_turned(k):
+        turn_copy(k).wait_recv()
+        work(k, other * 128, 64, other * 128)
 
     wait_bytes(buf.at[0, pl.ds(0, depth), pl.ds(0, 128)], block_sem.at[0])
+    work_own(0)
 
     def main(k, carry):
         wait_bytes(buf.at[0, pl.ds(0, depth * 3 // 2), :], block_sem.at[k])
@@ -233,13 +243,14 @@
         def _():
             send(k + lead)
 
-        work(k - 1)
+        work_own(k)
+        work_turned(k - 1)
         return carry
 
     lax.fori_loop(1, CHIPS, main, 0)
-    work(CHIPS - 1)
-
-    for phase in range(4):
+    work_turned(CHIPS - 1)
+
+    for phase in (2, 3):
         wait_phase(phase, phase_send)
     wait_bytes(buf.at[pl.ds(0, CHIPS - 1), pl.ds(0, depth), :], send_sem.at[0])
     wait_bytes(buf.at[:, pl.ds(0, depth), :], send_sem.at[1])
@@ -292,7 +303,7 @@
             pltpu.SemaphoreType.DMA((2,)),
             pltpu.SemaphoreType.DMA((CHIPS,)),
             pltpu.SemaphoreType.DMA((4,)),
-            pltpu.SemaphoreType.DMA((4, 2)),
+            pltpu.SemaphoreType.DMA((2, 2)),
             pltpu.SemaphoreType.DMA((4, 2)),
             pltpu.SemaphoreType.REGULAR((3,)),
             pltpu.SemaphoreType.DMA((5,)),

time: 120 us -> 120 us (level)
  no operation moved by 1% of the time
where the time goes in v4:
time: 120 us; the launch traced here: 119 us
  Pallas kernels  118 us (98%)
    pallas_call x1, Pallas kernels, shards(): pl.pallas_call(gather_kernel, out_shape=(jax.ShapeDtypeStruct((depth, inn...  116 us
    pallas_call x1, Pallas kernels, shards(): pl.pallas_call(scale_kernel, out_shape=(jax.ShapeDtypeStruct((depth, inne...  2.46 us

profile of v4, /device:TPU:1, one launch (start us, length us, event | category | flops | bytes accessed | tf_op | source)
XLA Modules:
  0.0 118.9 jit_solution(1925341010119824202)
XLA Ops:
  0.6 115.8 %gather.1 = (f32[192,12288]{1,0:T(8,128)S(1)}, f32[192,128]{1,0:T(8,128)S(1)}, f32[96,128]{1,0:T(8,128)S(1)}) custom-call(bf16[192,12288]{1,0:T(8,128)(2,1)} %weight.1, bf16[64,192]{1,0:T(8,128)(2,1)} %bitcast.6, bf16[64,12288]{1,0:T(8,128)(2,1)} %high.1, f32[1,48]{1,0:T(1,128)} %bitcast.7, f32[1,48]{1,0:T(1,128)} %bitcast.8), custom_call_target="tpu_custom_call" | custom-call | tf_op jit(solution)/shard_map/gather/pallas_call | solution.py:286
  116.4 2.5 %scale.1 = (bf16[192,12288]{1,0:T(8,128)(2,1)}, f32[1,192]{1,0:T(1,128)}, bf16[96,128]{1,0:T(8,128)(2,1)}) custom-call(f32[192,12288]{1,0:T(8,128)S(1)} %get-tuple-element.9.latest, f32[192,128]{1,0:T(8,128)S(1)} %get-tuple-element.10.tops, f32[96,128]{1,0:T(8,128)S(1)} %get-tuple-element.11.norm), custom_call_target="tpu_custom_call" | custom-call | tf_op jit(solution)/shard_map/scale/pallas_call | solution.py:319
